TPU v7x, 32 devices: a whole 2x2x4 slice. The times are simulated.
32 devices in a mesh: row: 2 (over x), col: 16 (over z, y, core).
Axes of the slice: x: 2, y: 2, z: 4, core: 2. Of those that a mesh axis runs over, the one named last changes fastest.
Arguments:
- eigvecs: float32 [16384, 4096], P('row', 'col'), may hold values from -6 to 6
- v_panels: float32 [8, 16384, 256], P(None, 'row', 'col'), as said below
- t_panels: float32 [8, 256, 256], P(None, None, 'col'), as said below
Outputs:
- rotated: float32 [16384, 4096], P('row', 'col')
Inputs may be any that keep to these rules, and one draw needn't show every extreme that they name: `v_panels`: in panel k, vector j is zero in rows above k * 256 + j + 1, equals 1 in that row and is dense below it. t_panels[k] is upper triangular and V_k t_panels[k] V_k^T = I minus the product of the panel's 256 Householder reflections, each I - 2 v v^T / (v^T v), taken in the order of j; its diagonal lies in (0, 2].
All inputs are finite; a program needn't handle non-finite values.
Results may differ from a plain program's by a relative error of at most 0.00015.
Values sent between devices are 32-bit elements; how exact they have to be, the bound alone decides.
A program may use at most 192 MiB of HBM per device.

v0:
```python
import functools

import jax
import jax.numpy as jnp
from jax import lax
from jax.experimental import pallas as pl
from jax.experimental.pallas import tpu as pltpu
from jax.sharding import PartitionSpec as P

SLOTS = 4
MESH = pl.DeviceIdType.MESH


def halves(x):
    high = x.astype(jnp.bfloat16)
    return high, (x - high.astype(jnp.float32)).astype(jnp.bfloat16)


def dot3(left, right, left_axis, right_axis):
    def one(a, b):
        return lax.dot_general(
            a, b, (((left_axis,), (right_axis,)), ((), ())), preferred_element_type=jnp.float32
        )

    (lh, ll), (rh, rl) = left, right
    return one(lh, rh) + (one(ll, rh) + one(lh, rl))


def kernel(shape, z_hbm, p_ref, out_ref, g_ref, zbuf, vbuf, acc, psend, precv, *sems):
    panels, width, rows, groups, A, B = shape
    recv, su, sd, sy, sc, lsem, zsem, psnd, prcv = sems
    per = p_ref.shape[1]
    length = p_ref.shape[2]
    tiles = length // 128
    cut = (tiles - tiles // 4) * 128
    lanes = (pl.ds(0, cut), pl.ds(cut, length - cut))
    tile = min(rows, 1024)
    me = lax.axis_index("col")
    my_row = lax.axis_index("row")
    c = lax.rem(me, 2)
    b = lax.rem(me // 2, B)
    a = me // (2 * B)

    def index(aa, bb, cc):
        return (aa * B + bb) * 2 + cc

    def walk(i, s, go):
        k = panels - 1 - i
        sl = lax.rem(i, SLOTS)

        def place(owner, q):
            return g_ref.at[k, pl.ds(pl.multiple_of(owner * per, per), per), lanes[q]]

        def move(owner, q, own, target, sem):
            copy = pltpu.make_async_remote_copy(
                src_ref=p_ref.at[k, :, lanes[q]] if own else place(owner, q),
                dst_ref=place(owner, q),
                send_sem=sem,
                recv_sem=recv.at[sl, q, owner],
                device_id={"col": target},
                device_id_type=MESH,
            )
            if go:
                copy.start()
            else:
                copy.wait_send()

        def arrive(owner, q):
            if go:
                pltpu.make_async_remote_copy(
                    src_ref=place(owner, q),
                    dst_ref=place(owner, q),
                    send_sem=sc.at[sl, q, 0],
                    recv_sem=recv.at[sl, q, owner],
                    device_id={"col": index(a, b, 1 - c)},
                    device_id_type=MESH,
                ).wait_recv()

        def along(sg, owner, q, own, cid):
            if sg >= 0:

                @pl.when(a < A - 1)
                def _():
                    move(owner, q, own, index(a + 1, b, c), su.at[sl, q, cid])

            if sg <= 0:

                @pl.when(a > 0)
                def _():
                    move(owner, q, own, index(a - 1, b, c), sd.at[sl, q, cid])

        def across(owner, q, own, slot):
            for j in range(1, B):
                move(owner, q, own, index(a, lax.rem(b + j, B), c), sy.at[sl, slot, j - 1])

        def over(owner, q, own, cid):
            move(owner, q, own, index(a, b, 1 - c), sc.at[sl, q, cid])

        def signs(d):
            return (1, -1) if d else (0,)

        if s < A:
            for sg in signs(s):
                at = a - sg * s

                @pl.when((at >= 0) & (at < A))
                def _(sg=sg, at=at):
                    owner, cid, own = index(at, b, c), at * B + b, s == 0
                    if not own:
                        arrive(owner, 0)
                    along(sg, owner, 0, own, cid)
                    across(owner, 0, own, at)
                    over(owner, 0, own, cid)

        if s == 0:
            across(me, 1, True, A)
            along(0, me, 1, True, a * B + b)
            over(me, 1, True, a * B + b)
        else:
            for sg in signs(s - 1):
                at = a - sg * (s - 1)

                @pl.when((at >= 0) & (at < A))
                def _(sg=sg, at=at):
                    for j in range(B):
                        if s == 1 and j == 0:
                            continue
                        bb = lax.rem(b + j, B)
                        owner, cid = index(at, bb, c), at * B + bb
                        arrive(owner, 1)
                        along(sg, owner, 1, False, cid)
                        over(owner, 1, False, cid)
                    for j in range(1, B):
                        bb = lax.rem(b + j, B)
                        owner, cid = index(at, bb, c), at * B + bb
                        arrive(owner, 0)
                        over(owner, 0, False, cid)

    def settle(i):
        k = panels - 1 - i
        sl = lax.rem(i, SLOTS)
        for at in range(A):
            for bb in range(B):
                owner = index(at, bb, 1 - c)
                for q in range(2):
                    spot = g_ref.at[k, pl.ds(pl.multiple_of(owner * per, per), per), lanes[q]]
                    pltpu.make_async_remote_copy(
                        src_ref=spot,
                        dst_ref=spot,
                        send_sem=sc.at[sl, q, 0],
                        recv_sem=recv.at[sl, q, owner],
                        device_id={"col": index(a, b, 1 - c)},
                        device_id_type=MESH,
                    ).wait_recv()

    def load(i):
        k = panels - 1 - i
        sl = lax.rem(i, 2)
        for owner in range(A * B * 2):
            spot = pl.ds(owner * per, per)

            @pl.when(me == owner)
            def _():
                pltpu.make_async_copy(p_ref.at[k], vbuf.at[sl, spot], lsem.at[sl]).start()

            @pl.when(me != owner)
            def _():
                pltpu.make_async_copy(g_ref.at[k, spot], vbuf.at[sl, spot], lsem.at[sl]).start()

    def partial(sl, j):
        return pltpu.make_async_remote_copy(
            src_ref=psend.at[sl],
            dst_ref=precv.at[sl, j - 1],
            send_sem=psnd.at[sl, j - 1],
            recv_sem=prcv.at[sl, j - 1],
            device_id={"row": lax.rem(my_row + j, groups)},
            device_id_type=MESH,
        )

    def project(i):
        k = panels - 1 - i
        sl = lax.rem(i, 2)
        pltpu.make_async_copy(g_ref.at[k], vbuf.at[sl], lsem.at[sl]).wait()
        acc[...] = jnp.zeros_like(acc)

        def body(n, _):
            at = pl.multiple_of(n * tile, tile)
            left = halves(vbuf[sl, :, pl.ds(at, tile)])
            right = halves(zbuf[pl.ds(at, tile), :])
            acc[...] += dot3(left, right, 1, 0)
            return 0

        lax.fori_loop(0, rows // tile, body, 0)
        psend[sl] = acc[...]
        for j in range(1, groups):
            partial(sl, j).start()

    def store(n):
        spot = pl.ds(pl.multiple_of(n * tile, tile), tile)
        return pltpu.make_async_copy(zbuf.at[spot], out_ref.at[spot], zsem)

    def update(i):
        sl = lax.rem(i, 2)
        total = acc[...]
        for j in range(1, groups):
            partial(sl, j).wait()
            total = total + precv[sl, j - 1]
        factor = halves(vbuf[sl, :, pl.ds(rows, width)])
        scaled = halves(dot3(factor, halves(total), 0, 0))

        def body(n, _):
            at = pl.multiple_of(n * tile, tile)
            left = halves(vbuf[sl, :, pl.ds(at, tile)])
            zbuf[pl.ds(at, tile), :] = zbuf[pl.ds(at, tile), :] - dot3(left, scaled, 0, 0)

            @pl.when((i == panels - 1) & (n > 0))
            def _():
                store(n - 1).start()

            return 0

        lax.fori_loop(0, rows // tile, body, 0)

    fetch = pltpu.make_async_copy(z_hbm, zbuf, zsem)
    fetch.start()
    walk(0, 0, True)
    fetch.wait()

    def iteration(i, _):
        @pl.when(i < panels)
        def _():
            walk(i, 1, True)

        @pl.when(i > 0)
        def _():
            walk(i - 1, A, True)

        @pl.when(i + 1 < panels)
        def _():
            walk(i + 1, 0, True)

        @pl.when(i > 0)
        def _():
            settle(i - 1)
            load(i - 1)

        @pl.when(i < panels)
        def _():
            for s in range(2, A - 1):
                walk(i, s, True)

        @pl.when(i > 0)
        def _():
            project(i - 1)

        @pl.when(i < panels)
        def _():
            walk(i, A - 1, True)

        @pl.when(i > 0)
        def _():
            update(i - 1)

        @pl.when(i > 0)
        def _():
            for s in range(A + 1):
                walk(i - 1, s, False)

        return 0

    lax.fori_loop(0, panels + 1, iteration, 0)
    store(rows // tile - 1).start()
    pltpu.make_async_copy(zbuf, out_ref, zsem).wait()


def local(eigvecs, v_panels, t_panels):
    panels, rows, per = v_panels.shape
    width = t_panels.shape[1]
    groups = lax.axis_size("row")
    members = lax.axis_size("col")
    chips = members // 2
    B = max(n for n in range(1, chips + 1) if chips % n == 0 and n * n <= chips)
    A = chips // B
    columns = eigvecs.shape[1]
    packed = jnp.concatenate(
        [jnp.transpose(v_panels, (0, 2, 1)), jnp.transpose(t_panels, (0, 2, 1))], axis=2
    )
    length = rows + width
    dma = pltpu.SemaphoreType.DMA
    anywhere = pl.BlockSpec(memory_space=pl.ANY)
    others = max(groups - 1, 1)
    out, _ = pl.pallas_call(
        functools.partial(kernel, (panels, width, rows, groups, A, B)),
        out_shape=(
            jax.ShapeDtypeStruct((rows, columns), jnp.float32),
            jax.ShapeDtypeStruct((panels, width, length), jnp.float32),
        ),
        in_specs=[anywhere] * 2,
        out_specs=(anywhere, anywhere),
        scratch_shapes=[
            pltpu.VMEM((rows, columns), jnp.float32),
            pltpu.VMEM((2, width, length), jnp.float32),
            pltpu.VMEM((width, columns), jnp.float32),
            pltpu.VMEM((2, width, columns), jnp.float32),
            pltpu.VMEM((2, others, width, columns), jnp.float32),
            dma((SLOTS, 2, members)),
            dma((SLOTS, 2, chips)),
            dma((SLOTS, 2, chips)),
            dma((SLOTS, A + 1, max(B - 1, 1))),
            dma((SLOTS, 2, chips)),
            dma((2,)),
            dma,
            dma((2, others)),
            dma((2, others)),
        ],
        compiler_params=pltpu.CompilerParams(has_side_effects=True, vmem_limit_bytes=60 * 2**20),
    )(eigvecs, packed)
    return out


def solution(mesh):
    in_specs = (P("row", "col"), P(None, "row", "col"), P(None, None, "col"))
    out_specs = P("row", "col")
    return jax.shard_map(local, mesh=mesh, in_specs=in_specs, out_specs=out_specs, check_vma=False)
```

profile of v0, /device:TPU:0, one launch (start us, length us, event | category | flops | bytes accessed | tf_op | source)
XLA Modules:
  0.0 394.9 jit_solution(7626380581532824363)
XLA Ops:
  0.0 4.7 %pad_maximum_fusion.p_ref = f32[8,16,8448]{2,1,0:T(8,128)} fusion(f32[8,16,256]{2,1,0:T(8,128)} %bitcast.3, f32[8,16,8192]{2,1,0:T(8,128)} %bitcast.2), kind=kLoop, calls=%fused_computation | loop fusion | flops 1081344 | bytes 8650752 | tf_op jit(solution)/shard_map/concatenate | solution.py:285
  4.7 382.9 %shard_map.37 = (f32[8192,256]{1,0:T(8,128)}, f32[8,256,8448]{2,1,0:T(8,128)}) custom-call(f32[8192,256]{1,0:T(8,128)} %z_hbm.1, f32[8,16,8448]{2,1,0:T(8,128)} %pad_maximum_fusion.p_ref), custom_call_target="tpu_custom_call" | custom-call | tf_op jit(solution)/shard_map/pallas_call | solution.py:292
  387.6 7.3 %copy.5 = f32[8192,256]{1,0:T(8,128)} copy(f32[8192,256]{1,0:T(8,128)} %get-tuple-element.6) | data formatting | bytes 16777216
where the time goes:
time: 396 us; the launch traced here: 395 us
  Pallas kernels  383 us (97%)
  local copies, waits for them, and re-layouts  7.32 us (2%)
  other arithmetic  4.69 us (1%)
    pallas_call x1, Pallas kernels, local(): pl.pallas_call(functools.partial(kernel, (panels, width, rows, groups, A,...  383 us

commit v1 on v0

v1 whole, which is shorter than its diff:
```python
import functools

import jax
import jax.numpy as jnp
from jax import lax
from jax.experimental import pallas as pl
from jax.experimental.pallas import tpu as pltpu
from jax.sharding import PartitionSpec as P

SLOTS = 8
AHEAD = 2
MESH = pl.DeviceIdType.MESH


def halves(x):
    high = x.astype(jnp.bfloat16)
    return high, (x - high.astype(jnp.float32)).astype(jnp.bfloat16)


def dot3(left, right, left_axis, right_axis):
    def one(a, b):
        return lax.dot_general(
            a, b, (((left_axis,), (right_axis,)), ((), ())), preferred_element_type=jnp.float32
        )

    (lh, ll), (rh, rl) = left, right
    return one(lh, rh) + (one(ll, rh) + one(lh, rl))


def kernel(shape, z_hbm, v_ref, t_ref, out_ref, g_ref, gt_ref, zbuf, vbuf, tbuf, acc, psend, precv, *sems):
    groups, A, B = shape
    recv, su, sd, sy, sc, lsem, zsem, psnd, prcv, town, tsnd, trcv, tlsem = sems
    panels, H, sub, rows = v_ref.shape
    members = 2 * A * B
    width = H * members * sub
    units = panels * H
    share = panels // groups
    tiles = rows // 128
    spare = (B - 1) * A - (A - 1)
    whole = 2 * max((A - 1) * (B - 1), 1)
    side = min(max((tiles * spare + whole // 2) // whole, 1), tiles - 1)
    cut = (tiles - side) * 128
    lanes = (pl.ds(0, cut), pl.ds(cut, rows - cut))
    tile = min(rows, 1024)
    me = lax.axis_index("col")
    my_row = lax.axis_index("row")
    c = lax.rem(me, 2)
    b = lax.rem(me // 2, B)
    a = me // (2 * B)
    mine = pl.ds(my_row * share, share)

    def index(aa, bb, cc):
        return (aa * B + bb) * 2 + cc

    def place(u, owner, q):
        if q == 2:
            return gt_ref.at[mine, :, owner]
        return g_ref.at[panels - 1 - u // H, lax.rem(u, H), owner, :, lanes[q]]

    def first(u, q):
        if q == 2:
            return t_ref.at[mine]
        return v_ref.at[panels - 1 - u // H, lax.rem(u, H), :, lanes[q]]

    def landed(u, owner, q):
        sl = lax.rem(u, SLOTS)
        spot = place(u, owner, q)
        pltpu.make_async_remote_copy(
            src_ref=spot,
            dst_ref=spot,
            send_sem=sc.at[sl, q, 0],
            recv_sem=recv.at[sl, q, owner],
            device_id={"col": index(a, b, 1 - c)},
            device_id_type=MESH,
        ).wait_recv()

    def hop(u, h, go):
        sl = lax.rem(u, SLOTS)

        def move(owner, q, own, target, sem):
            copy = pltpu.make_async_remote_copy(
                src_ref=first(u, q) if own else place(u, owner, q),
                dst_ref=place(u, owner, q),
                send_sem=sem,
                recv_sem=recv.at[sl, q, owner],
                device_id={"col": target},
                device_id_type=MESH,
            )
            if go:
                copy.start()
            else:
                copy.wait_send()

        def arrive(owner, q):
            if go:
                landed(u, owner, q)

        def along(sg, owner, q, own, cid):
            if sg >= 0:

                @pl.when(a < A - 1)
                def _():
                    move(owner, q, own, index(a + 1, b, c), su.at[sl, q, cid])

            if sg <= 0:

                @pl.when(a > 0)
                def _():
                    move(owner, q, own, index(a - 1, b, c), sd.at[sl, q, cid])

        def across(owner, q, own, slot):
            for j in range(1, B):
                move(owner, q, own, index(a, lax.rem(b + j, B), c), sy.at[sl, slot, j - 1])

        def over(owner, q, own, cid):
            move(owner, q, own, index(a, b, 1 - c), sc.at[sl, q, cid])

        def factors(body):
            pl.when(u == 0)(body)

        def signs(d):
            return (1, -1) if d else (0,)

        if h == 0:
            cid = a * B + b
            across(me, 1, True, A)
            along(0, me, 0, True, cid)
            along(0, me, 1, True, cid)
            across(me, 0, True, a)
            over(me, 0, True, cid)
            over(me, 1, True, cid)

            @factors
            def _():
                along(0, me, 2, True, cid)
                across(me, 2, True, A + 1 + a)
                over(me, 2, True, cid)

            return

        def facing(d, body):
            if d < A:
                for sg in signs(d):
                    at = a - sg * d
                    if d == 0:
                        body(sg, at)
                    else:
                        pl.when((at >= 0) & (at < A))(functools.partial(body, sg, at))

        def straight(sg, at):
            owner, cid = index(at, b, c), at * B + b
            arrive(owner, 0)
            along(sg, owner, 0, False, cid)
            across(owner, 0, False, at)
            over(owner, 0, False, cid)

            @factors
            def _():
                arrive(owner, 2)
                along(sg, owner, 2, False, cid)
                across(owner, 2, False, A + 1 + at)
                over(owner, 2, False, cid)

        def turned(sg, at):
            for j in range(1, B):
                bb = lax.rem(b + j, B)
                owner, cid = index(at, bb, c), at * B + bb
                arrive(owner, 1)
                along(sg, owner, 1, False, cid)
                over(owner, 1, False, cid)

        def beside(sg, at):
            owner, cid = index(at, b, c), at * B + b
            arrive(owner, 1)
            along(sg, owner, 1, False, cid)
            over(owner, 1, False, cid)

        def crossed(sg, at):
            for j in range(1, B):
                bb = lax.rem(b + j, B)
                owner, cid = index(at, bb, c), at * B + bb
                arrive(owner, 0)
                over(owner, 0, False, cid)

                @factors
                def _():
                    arrive(owner, 2)
                    over(owner, 2, False, cid)

        facing(h, straight)
        facing(h - 1, turned)
        facing(h, beside)
        facing(h - 1, crossed)

    def pass_factors(j):
        return pltpu.make_async_remote_copy(
            src_ref=gt_ref.at[mine],
            dst_ref=gt_ref.at[mine],
            send_sem=tsnd.at[j - 1],
            recv_sem=trcv.at[j - 1],
            device_id={"row": lax.rem(my_row + j, groups)},
            device_id_type=MESH,
        )

    def own_factors():
        return pltpu.make_async_copy(t_ref.at[mine], gt_ref.at[mine, :, me], town)

    def settle(u):
        for at in range(A):
            for bb in range(B):
                for q in range(2):
                    landed(u, index(at, bb, 1 - c), q)

        @pl.when(u == 0)
        def _():
            for at in range(A):
                for bb in range(B):
                    landed(u, index(at, bb, 1 - c), 2)
            own_factors().wait()
            for j in range(1, groups):
                pass_factors(j).start()

    def load(u):
        k, h = panels - 1 - u // H, lax.rem(u, H)
        sl = lax.rem(u, 2 * H)
        pltpu.make_async_copy(v_ref.at[k, h], vbuf.at[sl, me], lsem.at[sl]).start()
        for j in range(1, members):
            owner = lax.rem(me + j, members)
            pltpu.make_async_copy(g_ref.at[k, h, owner], vbuf.at[sl, owner], lsem.at[sl]).start()

    def load_factor(i):
        @pl.when(i == 0)
        def _():
            for j in range(1, groups):
                pass_factors(j).wait_send()
                part = gt_ref.at[pl.ds(lax.rem(my_row + groups - j, groups) * share, share)]
                pltpu.make_async_remote_copy(
                    src_ref=part,
                    dst_ref=part,
                    send_sem=tsnd.at[j - 1],
                    recv_sem=trcv.at[j - 1],
                    device_id={"row": lax.rem(my_row + j, groups)},
                    device_id_type=MESH,
                ).wait_recv()

        return pltpu.make_async_copy(gt_ref.at[panels - 1 - i], tbuf, tlsem).start()

    def partial(sl, j):
        return pltpu.make_async_remote_copy(
            src_ref=psend.at[sl],
            dst_ref=precv.at[sl, j - 1],
            send_sem=psnd.at[sl, j - 1],
            recv_sem=prcv.at[sl, j - 1],
            device_id={"row": lax.rem(my_row + j, groups)},
            device_id_type=MESH,
        )

    def project(u):
        k, h = panels - 1 - u // H, lax.rem(u, H)
        sl = lax.rem(u, 2 * H)
        pltpu.make_async_copy(g_ref.at[k, h], vbuf.at[sl], lsem.at[sl]).wait()
        part = pl.ds(0, members * sub)
        acc[part] = jnp.zeros((members * sub, acc.shape[1]), jnp.float32)

        def body(n, _):
            at = pl.multiple_of(n * tile, tile)
            left = halves(vbuf[sl, :, :, pl.ds(at, tile)].reshape(members * sub, tile))
            right = halves(zbuf[pl.ds(at, tile), :])
            acc[part] += dot3(left, right, 1, 0)
            return 0

        lax.fori_loop(0, rows // tile, body, 0)
        psend[sl] = acc[part]
        for j in range(1, groups):
            partial(sl, j).start()

    def store(n):
        spot = pl.ds(pl.multiple_of(n * tile, tile), tile)
        return pltpu.make_async_copy(zbuf.at[spot], out_ref.at[spot], zsem)

    def update(i, last):
        base = lax.rem(i, 2) * H
        total = []
        for h in range(H):
            whole_sum = psend[base + h]
            for j in range(1, groups):
                partial(base + h, j).wait()
                whole_sum = whole_sum + precv[base + h, j - 1]
            total.append(whole_sum)
        total = halves(jnp.concatenate(total, axis=0))
        pltpu.make_async_copy(gt_ref.at[panels - 1 - i], tbuf, tlsem).wait()
        factor = halves(tbuf[...].reshape(width, width))
        scaled = dot3(factor, total, 0, 0)
        for h in range(H):
            for owner in range(members):
                at = (owner * H + h) * sub
                acc[pl.ds((h * members + owner) * sub, sub), :] = scaled[at : at + sub]
        scaled = halves(acc[...])

        def body(n, _):
            at = pl.multiple_of(n * tile, tile)
            left = halves(vbuf[pl.ds(base, H), :, :, pl.ds(at, tile)].reshape(width, tile))
            zbuf[pl.ds(at, tile), :] = zbuf[pl.ds(at, tile), :] - dot3(left, scaled, 0, 0)
            if last:

                @pl.when(n > 0)
                def _():
                    store(n - 1).start()

            return 0

        lax.fori_loop(0, rows // tile, body, 0)

    fetch = pltpu.make_async_copy(z_hbm, zbuf, zsem)
    fetch.start()
    for u in range(AHEAD):
        hop(jnp.int32(u), 0, True)
    own_factors().start()
    fetch.wait()

    def slot(t, _):
        w = t - A

        @pl.when(w >= 0)
        def _():
            i, h = w // H, lax.rem(w, H)

            @pl.when((h == 0) & (w > 0))
            def _():
                update(i - 1, False)

            @pl.when(h == H - 1)
            def _():
                load_factor(i)

            project(w)

        for h in range(A, 0, -1):
            u = t - (h - 1)

            @pl.when((u >= 0) & (u < units))
            def _(u=u, h=h):
                hop(u, h, True)

        @pl.when(t + AHEAD < units)
        def _():
            hop(t + AHEAD, 0, True)

        v = t - A + 1

        @pl.when((v >= 0) & (v < units))
        def _():
            settle(v)
            load(v)

        @pl.when(w >= 0)
        def _():
            for h in range(A + 1):
                hop(w, h, False)

        return 0

    lax.fori_loop(0, units + A, slot, 0)
    update(jnp.int32(panels - 1), True)
    store(rows // tile - 1).start()
    pltpu.make_async_copy(zbuf, out_ref, zsem).wait()


def local(eigvecs, v_panels, t_panels):
    panels, rows, per = v_panels.shape
    width = t_panels.shape[1]
    groups = lax.axis_size("row")
    members = lax.axis_size("col")
    chips = members // 2
    B = max(n for n in range(1, chips + 1) if chips % n == 0 and n * n <= chips)
    A = chips // B
    columns = eigvecs.shape[1]
    H = per // 8 if per % 8 == 0 else 1
    sub = per // H
    vectors = jnp.transpose(v_panels, (0, 2, 1)).reshape(panels, H, sub, rows)
    factors = jnp.transpose(t_panels, (0, 2, 1)).reshape(panels, H, sub, width)
    dma = pltpu.SemaphoreType.DMA
    anywhere = pl.BlockSpec(memory_space=pl.ANY)
    others = max(groups - 1, 1)
    out, _, _ = pl.pallas_call(
        functools.partial(kernel, (groups, A, B)),
        out_shape=(
            jax.ShapeDtypeStruct((rows, columns), jnp.float32),
            jax.ShapeDtypeStruct((panels, H, members, sub, rows), jnp.float32),
            jax.ShapeDtypeStruct((panels, H, members, sub, width), jnp.float32),
        ),
        in_specs=[anywhere] * 3,
        out_specs=(anywhere,) * 3,
        scratch_shapes=[
            pltpu.VMEM((rows, columns), jnp.float32),
            pltpu.VMEM((2 * H, members, sub, rows), jnp.float32),
            pltpu.VMEM((H, members, sub, width), jnp.float32),
            pltpu.VMEM((width, columns), jnp.float32),
            pltpu.VMEM((2 * H, members * sub, columns), jnp.float32),
            pltpu.VMEM((2 * H, others, members * sub, columns), jnp.float32),
            dma((SLOTS, 3, members)),
            dma((SLOTS, 3, chips)),
            dma((SLOTS, 3, chips)),
            dma((SLOTS, 2 * A + 1, max(B - 1, 1))),
            dma((SLOTS, 3, chips)),
            dma((2 * H,)),
            dma,
            dma((2 * H, others)),
            dma((2 * H, others)),
            dma,
            dma((others,)),
            dma((others,)),
            dma,
        ],
        compiler_params=pltpu.CompilerParams(has_side_effects=True, vmem_limit_bytes=60 * 2**20),
    )(eigvecs, vectors, factors)
    return out


def solution(mesh):
    in_specs = (P("row", "col"), P(None, "row", "col"), P(None, None, "col"))
    out_specs = P("row", "col")
    return jax.shard_map(local, mesh=mesh, in_specs=in_specs, out_specs=out_specs, check_vma=False)
```

time: 396 us -> 374 us (0.944)
  Pallas kernels: 383 us -> 366 us
  other arithmetic: 4.69 us -> 0 us
    pallas_call x1, Pallas kernels: 383 us -> 366 us  [local(): pl.pallas_call(functools.partial(kernel, (groups, A, B)), out_shape=(jax....]
    concatenate x1 -> x0, other arithmetic: 4.69 us -> none  [local(): jnp.concatenate([jnp.transpose(v_panels, (0, 2, 1)), jnp.transpose(t_pane...]
where the time goes in v1:
time: 374 us; the launch traced here: 373 us
  Pallas kernels  366 us (98%)
  local copies, waits for them, and re-layouts  7.32 us (2%)
    pallas_call x1, Pallas kernels, local(): pl.pallas_call(functools.partial(kernel, (groups, A, B)), out_shape=(jax....  366 us

profile of v1, /device:TPU:0, one launch (start us, length us, event | category | flops | bytes accessed | tf_op | source)
XLA Modules:
  0.0 373.4 jit_solution(6470089310649722879)
XLA Ops:
  0.0 366.1 %shard_map.37 = (f32[8192,256]{1,0:T(8,128)}, f32[8,2,16,8,8192]{4,3,2,1,0:T(8,128)}, f32[8,2,16,8,256]{4,3,2,1,0:T(8,128)}) custom-call(f32[8192,256]{1,0:T(8,128)} %z_hbm.1, f32[8,2,8,8192]{3,2,1,0:T(8,128)} %bitcast.6, f32[8,2,8,256]{3,2,1,0:T(8,128)} %bitcast.7), custom_call_target="tpu_custom_call" | custom-call | tf_op jit(solution)/shard_map/pallas_call | solution.py:385
  366.1 7.3 %copy.5 = f32[8192,256]{1,0:T(8,128)} copy(f32[8192,256]{1,0:T(8,128)} %get-tuple-element.6) | data formatting | bytes 16777216

commit v2 on v1

--- a/solution.py
+++ b/solution.py
@@ -27,11 +27,12 @@
     return one(lh, rh) + (one(ll, rh) + one(lh, rl))
 
 
-def kernel(shape, z_hbm, v_ref, t_ref, out_ref, g_ref, gt_ref, zbuf, vbuf, tbuf, acc, psend, precv, *sems):
+def kernel(shape, z_hbm, v_ref, t_ref, out_ref, zbuf, vbuf, tbuf, acc, psend, precv, *sems):
     groups, A, B = shape
-    recv, su, sd, sy, sc, lsem, zsem, psnd, prcv, town, tsnd, trcv, tlsem = sems
+    recv, su, sd, sy, sc, lsem, zsem, psnd, prcv, town, tsnd, trcv = sems
     panels, H, sub, rows = v_ref.shape
     members = 2 * A * B
+    ring = vbuf.shape[0]
     width = H * members * sub
     units = panels * H
     share = panels // groups
@@ -54,8 +55,8 @@
 
     def place(u, owner, q):
         if q == 2:
-            return gt_ref.at[mine, :, owner]
-        return g_ref.at[panels - 1 - u // H, lax.rem(u, H), owner, :, lanes[q]]
+            return tbuf.at[mine, :, owner]
+        return vbuf.at[lax.rem(u // H, ring), lax.rem(u, H), owner, :, lanes[q]]
 
     def first(u, q):
         if q == 2:
@@ -123,6 +124,8 @@
 
         if h == 0:
             cid = a * B + b
+            if go:
+                own_vectors(u).start()
             across(me, 1, True, A)
             along(0, me, 0, True, cid)
             along(0, me, 1, True, cid)
@@ -194,8 +197,8 @@
 
     def pass_factors(j):
         return pltpu.make_async_remote_copy(
-            src_ref=gt_ref.at[mine],
-            dst_ref=gt_ref.at[mine],
+            src_ref=tbuf.at[mine],
+            dst_ref=tbuf.at[mine],
             send_sem=tsnd.at[j - 1],
             recv_sem=trcv.at[j - 1],
             device_id={"row": lax.rem(my_row + j, groups)},
@@ -203,7 +206,7 @@
         )
 
     def own_factors():
-        return pltpu.make_async_copy(t_ref.at[mine], gt_ref.at[mine, :, me], town)
+        return pltpu.make_async_copy(t_ref.at[mine], tbuf.at[mine, :, me], town)
 
     def settle(u):
         for at in range(A):
@@ -220,30 +223,25 @@
             for j in range(1, groups):
                 pass_factors(j).start()
 
-    def load(u):
-        k, h = panels - 1 - u // H, lax.rem(u, H)
-        sl = lax.rem(u, 2 * H)
-        pltpu.make_async_copy(v_ref.at[k, h], vbuf.at[sl, me], lsem.at[sl]).start()
-        for j in range(1, members):
-            owner = lax.rem(me + j, members)
-            pltpu.make_async_copy(g_ref.at[k, h, owner], vbuf.at[sl, owner], lsem.at[sl]).start()
-
-    def load_factor(i):
-        @pl.when(i == 0)
-        def _():
-            for j in range(1, groups):
-                pass_factors(j).wait_send()
-                part = gt_ref.at[pl.ds(lax.rem(my_row + groups - j, groups) * share, share)]
-                pltpu.make_async_remote_copy(
-                    src_ref=part,
-                    dst_ref=part,
-                    send_sem=tsnd.at[j - 1],
-                    recv_sem=trcv.at[j - 1],
-                    device_id={"row": lax.rem(my_row + j, groups)},
-                    device_id_type=MESH,
-                ).wait_recv()
-
-        return pltpu.make_async_copy(gt_ref.at[panels - 1 - i], tbuf, tlsem).start()
+    def own_vectors(u):
+        return pltpu.make_async_copy(
+            v_ref.at[panels - 1 - u // H, lax.rem(u, H)],
+            vbuf.at[lax.rem(u // H, ring), lax.rem(u, H), me],
+            lsem.at[lax.rem(u, SLOTS)],
+        )
+
+    def swap_factors():
+        for j in range(1, groups):
+            pass_factors(j).wait_send()
+            part = tbuf.at[pl.ds(lax.rem(my_row + groups - j, groups) * share, share)]
+            pltpu.make_async_remote_copy(
+                src_ref=part,
+                dst_ref=part,
+                send_sem=tsnd.at[j - 1],
+                recv_sem=trcv.at[j - 1],
+                device_id={"row": lax.rem(my_row + j, groups)},
+                device_id_type=MESH,
+            ).wait_recv()
 
     def partial(sl, j):
         return pltpu.make_async_remote_copy(
@@ -256,15 +254,15 @@
         )
 
     def project(u):
-        k, h = panels - 1 - u // H, lax.rem(u, H)
+        spot, h = lax.rem(u // H, ring), lax.rem(u, H)
         sl = lax.rem(u, 2 * H)
-        pltpu.make_async_copy(g_ref.at[k, h], vbuf.at[sl], lsem.at[sl]).wait()
+        own_vectors(u).wait()
         part = pl.ds(0, members * sub)
         acc[part] = jnp.zeros((members * sub, acc.shape[1]), jnp.float32)
 
         def body(n, _):
             at = pl.multiple_of(n * tile, tile)
-            left = halves(vbuf[sl, :, :, pl.ds(at, tile)].reshape(members * sub, tile))
+            left = halves(vbuf[spot, h, :, :, pl.ds(at, tile)].reshape(members * sub, tile))
             right = halves(zbuf[pl.ds(at, tile), :])
             acc[part] += dot3(left, right, 1, 0)
             return 0
@@ -288,8 +286,8 @@
                 whole_sum = whole_sum + precv[base + h, j - 1]
             total.append(whole_sum)
         total = halves(jnp.concatenate(total, axis=0))
-        pltpu.make_async_copy(gt_ref.at[panels - 1 - i], tbuf, tlsem).wait()
-        factor = halves(tbuf[...].reshape(width, width))
+        spot = lax.rem(i, ring)
+        factor = halves(tbuf[panels - 1 - i].reshape(width, width))
         scaled = dot3(factor, total, 0, 0)
         for h in range(H):
             for owner in range(members):
@@ -299,7 +297,7 @@
 
         def body(n, _):
             at = pl.multiple_of(n * tile, tile)
-            left = halves(vbuf[pl.ds(base, H), :, :, pl.ds(at, tile)].reshape(width, tile))
+            left = halves(vbuf[spot, :, :, :, pl.ds(at, tile)].reshape(width, tile))
             zbuf[pl.ds(at, tile), :] = zbuf[pl.ds(at, tile), :] - dot3(left, scaled, 0, 0)
             if last:
 
@@ -325,14 +323,14 @@
         def _():
             i, h = w // H, lax.rem(w, H)
 
+            @pl.when((h == 0) & (i == 1))
+            def _():
+                swap_factors()
+
             @pl.when((h == 0) & (w > 0))
             def _():
                 update(i - 1, False)
 
-            @pl.when(h == H - 1)
-            def _():
-                load_factor(i)
-
             project(w)
 
         for h in range(A, 0, -1):
@@ -351,7 +349,6 @@
         @pl.when((v >= 0) & (v < units))
         def _():
             settle(v)
-            load(v)
 
         @pl.when(w >= 0)
         def _():
@@ -382,19 +379,16 @@
     dma = pltpu.SemaphoreType.DMA
     anywhere = pl.BlockSpec(memory_space=pl.ANY)
     others = max(groups - 1, 1)
-    out, _, _ = pl.pallas_call(
+    ring = min(panels, 1 + (A + AHEAD + 2 + H - 1) // H)
+    out = pl.pallas_call(
         functools.partial(kernel, (groups, A, B)),
-        out_shape=(
-            jax.ShapeDtypeStruct((rows, columns), jnp.float32),
-            jax.ShapeDtypeStruct((panels, H, members, sub, rows), jnp.float32),
-            jax.ShapeDtypeStruct((panels, H, members, sub, width), jnp.float32),
-        ),
+        out_shape=jax.ShapeDtypeStruct((rows, columns), jnp.float32),
         in_specs=[anywhere] * 3,
-        out_specs=(anywhere,) * 3,
+        out_specs=anywhere,
         scratch_shapes=[
             pltpu.VMEM((rows, columns), jnp.float32),
-            pltpu.VMEM((2 * H, members, sub, rows), jnp.float32),
-            pltpu.VMEM((H, members, sub, width), jnp.float32),
+            pltpu.VMEM((ring, H, members, sub, rows), jnp.float32),
+            pltpu.VMEM((panels, H, members, sub, width), jnp.float32),
             pltpu.VMEM((width, columns), jnp.float32),
             pltpu.VMEM((2 * H, members * sub, columns), jnp.float32),
             pltpu.VMEM((2 * H, others, members * sub, columns), jnp.float32),
@@ -403,16 +397,15 @@
             dma((SLOTS, 3, chips)),
             dma((SLOTS, 2 * A + 1, max(B - 1, 1))),
             dma((SLOTS, 3, chips)),
-            dma((2 * H,)),
+            dma((SLOTS,)),
             dma,
             dma((2 * H, others)),
             dma((2 * H, others)),
             dma,
             dma((others,)),
             dma((others,)),
-            dma,
         ],
-        compiler_params=pltpu.CompilerParams(has_side_effects=True, vmem_limit_bytes=60 * 2**20),
+        compiler_params=pltpu.CompilerParams(has_side_effects=True, vmem_limit_bytes=54 * 2**20),
     )(eigvecs, vectors, factors)
     return out
 

time: 374 us -> 371 us (level)
  no operation moved by 1% of the time
where the time goes in v2:
time: 371 us; the launch traced here: 370 us
  Pallas kernels  363 us (98%)
  local copies, waits for them, and re-layouts  7.32 us (2%)
    pallas_call x1, Pallas kernels, local(): pl.pallas_call(functools.partial(kernel, (groups, A, B)), out_shape=jax.S...  363 us

profile of v2, /device:TPU:0, one launch (start us, length us, event | category | flops | bytes accessed | tf_op | source)
XLA Modules:
  0.0 370.5 jit_solution(7076258113775293711)
XLA Ops:
  0.0 363.2 %shard_map.37 = f32[8192,256]{1,0:T(8,128)} custom-call(f32[8192,256]{1,0:T(8,128)} %z_hbm.1, f32[8,2,8,8192]{3,2,1,0:T(8,128)} %bitcast.6, f32[8,2,8,256]{3,2,1,0:T(8,128)} %bitcast.7), custom_call_target="tpu_custom_call" | custom-call | tf_op jit(solution)/shard_map/pallas_call | solution.py:383
  363.2 7.3 %copy.5 = f32[8192,256]{1,0:T(8,128)} copy(f32[8192,256]{1,0:T(8,128)} %shard_map.37) | data formatting | bytes 16777216

commit v3 on v2

--- a/solution.py
+++ b/solution.py
@@ -27,9 +27,10 @@
     return one(lh, rh) + (one(ll, rh) + one(lh, rl))
 
 
-def kernel(shape, z_hbm, v_ref, t_ref, out_ref, zbuf, vbuf, tbuf, acc, psend, precv, *sems):
-    groups, A, B = shape
-    recv, su, sd, sy, sc, lsem, zsem, psnd, prcv, town, tsnd, trcv = sems
+def kernel(shape, z_hbm, v_ref, t_ref, out_ref, zbuf, vbuf, tbuf, stage, acc, psend, precv, *sems):
+    groups, A, B, zone, tile = shape
+    recv, su, sd, sy, sc, lsem, zsem, psnd, prcv, town, tsnd, trcv = sems[:12]
+    lsnd, lrcv, gsnd, grcv = sems[12:]
     panels, H, sub, rows = v_ref.shape
     members = 2 * A * B
     ring = vbuf.shape[0]
@@ -41,8 +42,10 @@
     whole = 2 * max((A - 1) * (B - 1), 1)
     side = min(max((tiles * spare + whole // 2) // whole, 1), tiles - 1)
     cut = (tiles - side) * 128
-    lanes = (pl.ds(0, cut), pl.ds(cut, rows - cut))
-    tile = min(rows, 1024)
+    half = zone // 2
+    floor = zone // width
+    early = (panels - floor) * H if zone else 0
+    lanes = (pl.ds(half, cut - half), pl.ds(cut, rows - cut), None, pl.ds(0, half))
     me = lax.axis_index("col")
     my_row = lax.axis_index("row")
     c = lax.rem(me, 2)
@@ -58,10 +61,22 @@
             return tbuf.at[mine, :, owner]
         return vbuf.at[lax.rem(u // H, ring), lax.rem(u, H), owner, :, lanes[q]]
 
-    def first(u, q):
-        if q == 2:
-            return t_ref.at[mine]
-        return v_ref.at[panels - 1 - u // H, lax.rem(u, H), :, lanes[q]]
+    def source(u, span):
+        return v_ref.at[panels - 1 - u // H, lax.rem(u, H), :, span]
+
+    def slot_of(u, span):
+        return vbuf.at[lax.rem(u // H, ring), lax.rem(u, H), me, :, span]
+
+    def staged(u):
+        return stage.at[panels - 1 - u // H - floor, lax.rem(u, H)]
+
+    low, mid, high = pl.ds(0, half), pl.ds(half, zone - half), pl.ds(zone, rows - zone)
+
+    def lent(u, body):
+        if zone:
+            borrowed = (my_row == 0) & (u < early)
+            pl.when(borrowed)(lambda: body(staged(u)))
+            pl.when(jnp.logical_not(borrowed))(lambda: body(source(u, mid)))
 
     def landed(u, owner, q):
         sl = lax.rem(u, SLOTS)
@@ -75,70 +90,87 @@
             device_id_type=MESH,
         ).wait_recv()
 
-    def hop(u, h, go):
+    def hop(u, h, go, stages=(0, 1)):
         sl = lax.rem(u, SLOTS)
 
-        def move(owner, q, own, target, sem):
-            copy = pltpu.make_async_remote_copy(
-                src_ref=first(u, q) if own else place(u, owner, q),
-                dst_ref=place(u, owner, q),
-                send_sem=sem,
-                recv_sem=recv.at[sl, q, owner],
-                device_id={"col": target},
-                device_id_type=MESH,
-            )
-            if go:
-                copy.start()
+        def move(owner, q, own, target, sem, part=None):
+            def copy(src, dst):
+                return pltpu.make_async_remote_copy(
+                    src_ref=src,
+                    dst_ref=dst,
+                    send_sem=sem,
+                    recv_sem=recv.at[sl, q, owner],
+                    device_id={"col": target},
+                    device_id_type=MESH,
+                )
+
+            spot = place(u, owner, q)
+            if not go:
+                copy(spot, spot).wait_send()
+            elif not own:
+                copy(spot, spot).start()
+            elif part == "mid":
+                lent(u, lambda src: copy(src, slot_of(u, mid)).start())
+            elif q == 2:
+                copy(t_ref.at[mine], spot).start()
+            elif q == 0:
+                span = pl.ds(zone, cut - zone)
+                copy(source(u, span), slot_of(u, span)).start()
             else:
-                copy.wait_send()
+                copy(source(u, lanes[q]), spot).start()
 
         def arrive(owner, q):
             if go:
                 landed(u, owner, q)
 
-        def along(sg, owner, q, own, cid):
+        def along(sg, owner, q, own, cid, part=None):
             if sg >= 0:
 
                 @pl.when(a < A - 1)
                 def _():
-                    move(owner, q, own, index(a + 1, b, c), su.at[sl, q, cid])
+                    move(owner, q, own, index(a + 1, b, c), su.at[sl, q, cid], part)
 
             if sg <= 0:
 
                 @pl.when(a > 0)
                 def _():
-                    move(owner, q, own, index(a - 1, b, c), sd.at[sl, q, cid])
-
-        def across(owner, q, own, slot):
+                    move(owner, q, own, index(a - 1, b, c), sd.at[sl, q, cid], part)
+
+        def across(owner, q, own, at, part=None):
+            slot = (at, A, A + 1 + at, 2 * A + 1 + at)[q]
             for j in range(1, B):
-                move(owner, q, own, index(a, lax.rem(b + j, B), c), sy.at[sl, slot, j - 1])
-
-        def over(owner, q, own, cid):
-            move(owner, q, own, index(a, b, 1 - c), sc.at[sl, q, cid])
-
-        def factors(body):
-            pl.when(u == 0)(body)
+                move(owner, q, own, index(a, lax.rem(b + j, B), c), sy.at[sl, slot, j - 1], part)
+
+        def over(owner, q, own, cid, part=None):
+            move(owner, q, own, index(a, b, 1 - c), sc.at[sl, q, cid], part)
+
+        def extras(body):
+            pl.when(u == 0)(functools.partial(body, 2))
+            if zone:
+                pl.when(u >= early)(functools.partial(body, 3))
 
         def signs(d):
             return (1, -1) if d else (0,)
 
+        def spread(q, part=None):
+            cid = a * B + b
+            along(0, me, q, True, cid, part)
+            across(me, q, True, a, part)
+            over(me, q, True, cid, part)
+
         if h == 0:
-            cid = a * B + b
-            if go:
-                own_vectors(u).start()
-            across(me, 1, True, A)
-            along(0, me, 0, True, cid)
-            along(0, me, 1, True, cid)
-            across(me, 0, True, a)
-            over(me, 0, True, cid)
-            over(me, 1, True, cid)
-
-            @factors
-            def _():
-                along(0, me, 2, True, cid)
-                across(me, 2, True, A + 1 + a)
-                over(me, 2, True, cid)
-
+            if 0 in stages:
+                across(me, 1, True, a)
+                along(0, me, 0, True, a * B + b)
+                along(0, me, 1, True, a * B + b)
+                across(me, 0, True, a)
+                over(me, 0, True, a * B + b)
+                over(me, 1, True, a * B + b)
+                extras(spread)
+            if 1 in stages and go:
+                if zone:
+                    spread(0, "mid")
+                own_vectors(u)
             return
 
         def facing(d, body):
@@ -157,12 +189,12 @@
             across(owner, 0, False, at)
             over(owner, 0, False, cid)
 
-            @factors
-            def _():
-                arrive(owner, 2)
-                along(sg, owner, 2, False, cid)
-                across(owner, 2, False, A + 1 + at)
-                over(owner, 2, False, cid)
+            @extras
+            def _(q):
+                arrive(owner, q)
+                along(sg, owner, q, False, cid)
+                across(owner, q, False, at)
+                over(owner, q, False, cid)
 
         def turned(sg, at):
             for j in range(1, B):
@@ -185,10 +217,10 @@
                 arrive(owner, 0)
                 over(owner, 0, False, cid)
 
-                @factors
-                def _():
-                    arrive(owner, 2)
-                    over(owner, 2, False, cid)
+                @extras
+                def _(q):
+                    arrive(owner, q)
+                    over(owner, q, False, cid)
 
         facing(h, straight)
         facing(h - 1, turned)
@@ -214,6 +246,25 @@
                 for q in range(2):
                     landed(u, index(at, bb, 1 - c), q)
 
+        if zone:
+
+            @pl.when(u >= early)
+            def _():
+                for at in range(A):
+                    for bb in range(B):
+                        landed(u, index(at, bb, 1 - c), 3)
+                own_arrived(u, pl.ds(0, rows))
+
+            @pl.when(u < early)
+            def _():
+                own_arrived(u, pl.ds(half, rows - half))
+
+                @pl.when(my_row == 0)
+                def _():
+                    hand(u).start()
+        else:
+            own_arrived(u, pl.ds(0, rows))
+
         @pl.when(u == 0)
         def _():
             for at in range(A):
@@ -224,11 +275,41 @@
                 pass_factors(j).start()
 
     def own_vectors(u):
-        return pltpu.make_async_copy(
-            v_ref.at[panels - 1 - u // H, lax.rem(u, H)],
-            vbuf.at[lax.rem(u // H, ring), lax.rem(u, H), me],
-            lsem.at[lax.rem(u, SLOTS)],
+        sem = lsem.at[lax.rem(u, SLOTS)]
+        pltpu.make_async_copy(source(u, high), slot_of(u, high), sem).start()
+        if zone:
+            lent(u, lambda src: pltpu.make_async_copy(src, slot_of(u, mid), sem).start())
+
+            @pl.when(u >= early)
+            def _():
+                pltpu.make_async_copy(source(u, low), slot_of(u, low), sem).start()
+
+    def own_arrived(u, span):
+        pltpu.make_async_copy(source(u, span), slot_of(u, span), lsem.at[lax.rem(u, SLOTS)]).wait()
+
+    def lend():
+        return pltpu.make_async_remote_copy(
+            src_ref=v_ref.at[pl.ds(floor, panels - floor), :, :, low],
+            dst_ref=stage,
+            send_sem=lsnd,
+            recv_sem=lrcv,
+            device_id={"row": 1 - my_row},
+            device_id_type=MESH,
         )
+
+    def hand(u):
+        spot, h = lax.rem(u // H, ring), lax.rem(u, H)
+        return pltpu.make_async_remote_copy(
+            src_ref=vbuf.at[spot, h, :, :, mid],
+            dst_ref=vbuf.at[spot, h, :, :, low],
+            send_sem=gsnd.at[lax.rem(u, SLOTS)],
+            recv_sem=grcv.at[lax.rem(u, SLOTS)],
+            device_id={"row": 1 - my_row},
+            device_id_type=MESH,
+        )
+
+    def begin(u):
+        return jnp.where((my_row == 0) & (u < early), 1, 0) if zone else 0
 
     def swap_factors():
         for j in range(1, groups):
@@ -256,7 +337,12 @@
     def project(u):
         spot, h = lax.rem(u // H, ring), lax.rem(u, H)
         sl = lax.rem(u, 2 * H)
-        own_vectors(u).wait()
+        if zone:
+
+            @pl.when((my_row == 1) & (u < early))
+            def _():
+                hand(u).wait_recv()
+
         part = pl.ds(0, members * sub)
         acc[part] = jnp.zeros((members * sub, acc.shape[1]), jnp.float32)
 
@@ -267,7 +353,7 @@
             acc[part] += dot3(left, right, 1, 0)
             return 0
 
-        lax.fori_loop(0, rows // tile, body, 0)
+        lax.fori_loop(begin(u), rows // tile, body, 0)
         psend[sl] = acc[part]
         for j in range(1, groups):
             partial(sl, j).start()
@@ -307,13 +393,27 @@
 
             return 0
 
-        lax.fori_loop(0, rows // tile, body, 0)
+        lax.fori_loop(0 if last else begin(i * H), rows // tile, body, 0)
 
     fetch = pltpu.make_async_copy(z_hbm, zbuf, zsem)
+    if zone:
+
+        @pl.when(my_row == 1)
+        def _():
+            lend().start()
+
+    for u in range(AHEAD):
+        hop(jnp.int32(u), 0, True, (0,))
     fetch.start()
+    own_factors().start()
+    if zone:
+
+        @pl.when(my_row == 0)
+        def _():
+            lend().wait_recv()
+
     for u in range(AHEAD):
-        hop(jnp.int32(u), 0, True)
-    own_factors().start()
+        hop(jnp.int32(u), 0, True, (1,))
     fetch.wait()
 
     def slot(t, _):
@@ -354,11 +454,22 @@
         def _():
             for h in range(A + 1):
                 hop(w, h, False)
+            if zone:
+
+                @pl.when((my_row == 0) & (w < early))
+                def _():
+                    hand(w).wait_send()
 
         return 0
 
     lax.fori_loop(0, units + A, slot, 0)
     update(jnp.int32(panels - 1), True)
+    if zone:
+
+        @pl.when(my_row == 1)
+        def _():
+            lend().wait_send()
+
     store(rows // tile - 1).start()
     pltpu.make_async_copy(zbuf, out_ref, zsem).wait()
 
@@ -380,8 +491,11 @@
     anywhere = pl.BlockSpec(memory_space=pl.ANY)
     others = max(groups - 1, 1)
     ring = min(panels, 1 + (A + AHEAD + 2 + H - 1) // H)
+    tile = min(rows, 1024)
+    zone = tile if groups == 2 and rows >= 4 * tile and tile % (2 * width) == 0 and tile < panels * width else 0
+    lent = (panels - zone // width, H, sub, zone // 2) if zone else (1, H, sub, 128)
     out = pl.pallas_call(
-        functools.partial(kernel, (groups, A, B)),
+        functools.partial(kernel, (groups, A, B, zone, tile)),
         out_shape=jax.ShapeDtypeStruct((rows, columns), jnp.float32),
         in_specs=[anywhere] * 3,
         out_specs=anywhere,
@@ -389,14 +503,15 @@
             pltpu.VMEM((rows, columns), jnp.float32),
             pltpu.VMEM((ring, H, members, sub, rows), jnp.float32),
             pltpu.VMEM((panels, H, members, sub, width), jnp.float32),
+            pltpu.VMEM(lent, jnp.float32),
             pltpu.VMEM((width, columns), jnp.float32),
             pltpu.VMEM((2 * H, members * sub, columns), jnp.float32),
             pltpu.VMEM((2 * H, others, members * sub, columns), jnp.float32),
-            dma((SLOTS, 3, members)),
-            dma((SLOTS, 3, chips)),
-            dma((SLOTS, 3, chips)),
-            dma((SLOTS, 2 * A + 1, max(B - 1, 1))),
-            dma((SLOTS, 3, chips)),
+            dma((SLOTS, 4, members)),
+            dma((SLOTS, 4, chips)),
+            dma((SLOTS, 4, chips)),
+            dma((SLOTS, 3 * A + 1, max(B - 1, 1))),
+            dma((SLOTS, 4, chips)),
             dma((SLOTS,)),
             dma,
             dma((2 * H, others)),
@@ -404,6 +519,10 @@
             dma,
             dma((others,)),
             dma((others,)),
+            dma,
+            dma,
+            dma((SLOTS,)),
+            dma((SLOTS,)),
         ],
         compiler_params=pltpu.CompilerParams(has_side_effects=True, vmem_limit_bytes=54 * 2**20),
     )(eigvecs, vectors, factors)

time: 371 us -> 370 us (level)
  no operation moved by 1% of the time
where the time goes in v3:
time: 370 us
  Pallas kernels  363 us (98%)
  local copies, waits for them, and re-layouts  7.32 us (2%)
    pallas_call x1, Pallas kernels, local(): pl.pallas_call(functools.partial(kernel, (groups, A, B, zone, tile)), out...  363 us

profile of v3, /device:TPU:0, one launch (start us, length us, event | category | flops | bytes accessed | tf_op | source)
XLA Modules:
  0.0 370.0 jit_solution(7783560557191222046)
XLA Ops:
  0.0 362.6 %shard_map.37 = f32[8192,256]{1,0:T(8,128)} custom-call(f32[8192,256]{1,0:T(8,128)} %z_hbm.1, f32[8,2,8,8192]{3,2,1,0:T(8,128)} %bitcast.6, f32[8,2,8,256]{3,2,1,0:T(8,128)} %bitcast.7), custom_call_target="tpu_custom_call" | custom-call | tf_op jit(solution)/shard_map/pallas_call | solution.py:497
  362.6 7.3 %copy.5 = f32[8192,256]{1,0:T(8,128)} copy(f32[8192,256]{1,0:T(8,128)} %shard_map.37) | data formatting | bytes 16777216

commit v4 on v3

--- a/solution.py
+++ b/solution.py
@@ -45,7 +45,6 @@
     half = zone // 2
     floor = zone // width
     early = (panels - floor) * H if zone else 0
-    lanes = (pl.ds(half, cut - half), pl.ds(cut, rows - cut), None, pl.ds(0, half))
     me = lax.axis_index("col")
     my_row = lax.axis_index("row")
     c = lax.rem(me, 2)
@@ -56,10 +55,18 @@
     def index(aa, bb, cc):
         return (aa * B + bb) * 2 + cc
 
-    def place(u, owner, q):
+    def place(u, owner, q, start=0):
         if q == 2:
             return tbuf.at[mine, :, owner]
-        return vbuf.at[lax.rem(u // H, ring), lax.rem(u, H), owner, :, lanes[q]]
+        span = pl.ds(cut, rows - cut) if q else pl.ds(start, cut - start)
+        return vbuf.at[lax.rem(u // H, ring), lax.rem(u, H), owner, :, span]
+
+    def sized(u, q, body):
+        if zone and q == 0:
+            pl.when(u < early)(lambda: body(half))
+            pl.when(u >= early)(lambda: body(0))
+        else:
+            body(0)
 
     def source(u, span):
         return v_ref.at[panels - 1 - u // H, lax.rem(u, H), :, span]
@@ -73,22 +80,24 @@
     low, mid, high = pl.ds(0, half), pl.ds(half, zone - half), pl.ds(zone, rows - zone)
 
     def lent(u, body):
-        if zone:
-            borrowed = (my_row == 0) & (u < early)
-            pl.when(borrowed)(lambda: body(staged(u)))
-            pl.when(jnp.logical_not(borrowed))(lambda: body(source(u, mid)))
+        borrowed = (my_row == 0) & (u < early)
+        pl.when(borrowed)(lambda: body(staged(u)))
 
     def landed(u, owner, q):
         sl = lax.rem(u, SLOTS)
-        spot = place(u, owner, q)
-        pltpu.make_async_remote_copy(
-            src_ref=spot,
-            dst_ref=spot,
-            send_sem=sc.at[sl, q, 0],
-            recv_sem=recv.at[sl, q, owner],
-            device_id={"col": index(a, b, 1 - c)},
-            device_id_type=MESH,
-        ).wait_recv()
+
+        def wait(start):
+            spot = place(u, owner, q, start)
+            pltpu.make_async_remote_copy(
+                src_ref=spot,
+                dst_ref=spot,
+                send_sem=sc.at[sl, q, 0],
+                recv_sem=recv.at[sl, q, owner],
+                device_id={"col": index(a, b, 1 - c)},
+                device_id_type=MESH,
+            ).wait_recv()
+
+        sized(u, q, wait)
 
     def hop(u, h, go, stages=(0, 1)):
         sl = lax.rem(u, SLOTS)
@@ -104,20 +113,27 @@
                     device_id_type=MESH,
                 )
 
-            spot = place(u, owner, q)
-            if not go:
-                copy(spot, spot).wait_send()
-            elif not own:
-                copy(spot, spot).start()
-            elif part == "mid":
+            def whole(start):
+                spot = place(u, owner, q, start)
+                if not go:
+                    copy(spot, spot).wait_send()
+                elif q == 2 and own:
+                    copy(t_ref.at[mine], spot).start()
+                elif own:
+                    span = pl.ds(cut, rows - cut) if q else pl.ds(start, cut - start)
+                    copy(source(u, span), spot).start()
+                else:
+                    copy(spot, spot).start()
+
+            if part == "mid":
                 lent(u, lambda src: copy(src, slot_of(u, mid)).start())
-            elif q == 2:
-                copy(t_ref.at[mine], spot).start()
-            elif q == 0:
-                span = pl.ds(zone, cut - zone)
-                copy(source(u, span), slot_of(u, span)).start()
+            elif zone and go and own and q == 0:
+                borrowed = (my_row == 0) & (u < early)
+                pl.when(borrowed)(lambda: whole(zone))
+                pl.when(jnp.logical_not(borrowed) & (u < early))(lambda: whole(half))
+                pl.when(u >= early)(lambda: whole(0))
             else:
-                copy(source(u, lanes[q]), spot).start()
+                sized(u, q, whole)
 
         def arrive(owner, q):
             if go:
@@ -137,17 +153,15 @@
                     move(owner, q, own, index(a - 1, b, c), sd.at[sl, q, cid], part)
 
         def across(owner, q, own, at, part=None):
-            slot = (at, A, A + 1 + at, 2 * A + 1 + at)[q]
+            slot = (at, A, A + 1 + at)[q]
             for j in range(1, B):
                 move(owner, q, own, index(a, lax.rem(b + j, B), c), sy.at[sl, slot, j - 1], part)
 
         def over(owner, q, own, cid, part=None):
             move(owner, q, own, index(a, b, 1 - c), sc.at[sl, q, cid], part)
 
-        def extras(body):
-            pl.when(u == 0)(functools.partial(body, 2))
-            if zone:
-                pl.when(u >= early)(functools.partial(body, 3))
+        def factors(body):
+            pl.when(u == 0)(body)
 
         def signs(d):
             return (1, -1) if d else (0,)
@@ -166,7 +180,7 @@
                 across(me, 0, True, a)
                 over(me, 0, True, a * B + b)
                 over(me, 1, True, a * B + b)
-                extras(spread)
+                factors(lambda: spread(2))
             if 1 in stages and go:
                 if zone:
                     spread(0, "mid")
@@ -189,12 +203,12 @@
             across(owner, 0, False, at)
             over(owner, 0, False, cid)
 
-            @extras
-            def _(q):
-                arrive(owner, q)
-                along(sg, owner, q, False, cid)
-                across(owner, q, False, at)
-                over(owner, q, False, cid)
+            @factors
+            def _():
+                arrive(owner, 2)
+                along(sg, owner, 2, False, cid)
+                across(owner, 2, False, at)
+                over(owner, 2, False, cid)
 
         def turned(sg, at):
             for j in range(1, B):
@@ -217,10 +231,10 @@
                 arrive(owner, 0)
                 over(owner, 0, False, cid)
 
-                @extras
-                def _(q):
-                    arrive(owner, q)
-                    over(owner, q, False, cid)
+                @factors
+                def _():
+                    arrive(owner, 2)
+                    over(owner, 2, False, cid)
 
         facing(h, straight)
         facing(h - 1, turned)
@@ -250,9 +264,6 @@
 
             @pl.when(u >= early)
             def _():
-                for at in range(A):
-                    for bb in range(B):
-                        landed(u, index(at, bb, 1 - c), 3)
                 own_arrived(u, pl.ds(0, rows))
 
             @pl.when(u < early)
@@ -275,14 +286,18 @@
                 pass_factors(j).start()
 
     def own_vectors(u):
-        sem = lsem.at[lax.rem(u, SLOTS)]
-        pltpu.make_async_copy(source(u, high), slot_of(u, high), sem).start()
+        def fetch_own(src, span):
+            pltpu.make_async_copy(src, slot_of(u, span), lsem.at[lax.rem(u, SLOTS)]).start()
+
         if zone:
-            lent(u, lambda src: pltpu.make_async_copy(src, slot_of(u, mid), sem).start())
-
-            @pl.when(u >= early)
-            def _():
-                pltpu.make_async_copy(source(u, low), slot_of(u, low), sem).start()
+            lent(u, lambda src: fetch_own(src, mid))
+            rest = pl.ds(half, rows - half)
+            borrowed = (my_row == 0) & (u < early)
+            pl.when(borrowed)(lambda: fetch_own(source(u, high), high))
+            pl.when(jnp.logical_not(borrowed) & (u < early))(lambda: fetch_own(source(u, rest), rest))
+            pl.when(u >= early)(lambda: fetch_own(source(u, pl.ds(0, rows)), pl.ds(0, rows)))
+        else:
+            fetch_own(source(u, pl.ds(0, rows)), pl.ds(0, rows))
 
     def own_arrived(u, span):
         pltpu.make_async_copy(source(u, span), slot_of(u, span), lsem.at[lax.rem(u, SLOTS)]).wait()
@@ -394,6 +409,21 @@
             return 0
 
         lax.fori_loop(0 if last else begin(i * H), rows // tile, body, 0)
+
+    barrier = pltpu.get_barrier_semaphore()
+
+    def greet(target):
+        pl.semaphore_signal(barrier, inc=1, device_id=target, device_id_type=MESH)
+
+    pl.when(a < A - 1)(lambda: greet({"col": index(a + 1, b, c)}))
+    pl.when(a > 0)(lambda: greet({"col": index(a - 1, b, c)}))
+    for j in range(1, B):
+        greet({"col": index(a, lax.rem(b + j, B), c)})
+    greet({"col": index(a, b, 1 - c)})
+    for j in range(1, groups):
+        greet({"row": lax.rem(my_row + j, groups)})
+    beyond = jnp.where(a < A - 1, 1, 0) + jnp.where(a > 0, 1, 0)
+    pl.semaphore_wait(barrier, beyond + (B + groups - 1))
 
     fetch = pltpu.make_async_copy(z_hbm, zbuf, zsem)
     if zone:
@@ -507,11 +537,11 @@
             pltpu.VMEM((width, columns), jnp.float32),
             pltpu.VMEM((2 * H, members * sub, columns), jnp.float32),
             pltpu.VMEM((2 * H, others, members * sub, columns), jnp.float32),
-            dma((SLOTS, 4, members)),
-            dma((SLOTS, 4, chips)),
-            dma((SLOTS, 4, chips)),
-            dma((SLOTS, 3 * A + 1, max(B - 1, 1))),
-            dma((SLOTS, 4, chips)),
+            dma((SLOTS, 3, members)),
+            dma((SLOTS, 3, chips)),
+            dma((SLOTS, 3, chips)),
+            dma((SLOTS, 2 * A + 1, max(B - 1, 1))),
+            dma((SLOTS, 3, chips)),
             dma((SLOTS,)),
             dma,
             dma((2 * H, others)),
@@ -524,7 +554,9 @@
             dma((SLOTS,)),
             dma((SLOTS,)),
         ],
-        compiler_params=pltpu.CompilerParams(has_side_effects=True, vmem_limit_bytes=54 * 2**20),
+        compiler_params=pltpu.CompilerParams(
+            collective_id=0, has_side_effects=True, vmem_limit_bytes=54 * 2**20
+        ),
     )(eigvecs, vectors, factors)
     return out
 

time: 370 us -> 360 us (0.973)
  Pallas kernels: 363 us -> 353 us
    pallas_call x1, Pallas kernels: 363 us -> 353 us  [local(): pl.pallas_call(functools.partial(kernel, (groups, A, B, zone, tile)), out...]
where the time goes in v4:
time: 360 us
  Pallas kernels  353 us (98%)
  local copies, waits for them, and re-layouts  7.32 us (2%)
    pallas_call x1, Pallas kernels, local(): pl.pallas_call(functools.partial(kernel, (groups, A, B, zone, tile)), out...  353 us
    unnamed x1, local copies, waits for them, and re-layouts  7.32 us

profile of v4, /device:TPU:0, one launch (start us, length us, event | category | flops | bytes accessed | tf_op | source)
XLA Modules:
  0.0 360.3 jit_solution(15952136852220635392)
XLA Ops:
  0.0 352.9 %shard_map.37 = f32[8192,256]{1,0:T(8,128)} custom-call(f32[8192,256]{1,0:T(8,128)} %z_hbm.1, f32[8,2,8,8192]{3,2,1,0:T(8,128)} %bitcast.6, f32[8,2,8,256]{3,2,1,0:T(8,128)} %bitcast.7), custom_call_target="tpu_custom_call" | custom-call | tf_op jit(solution)/shard_map/pallas_call | solution.py:527
  352.9 7.3 %copy.5 = f32[8192,256]{1,0:T(8,128)} copy(f32[8192,256]{1,0:T(8,128)} %shard_map.37) | data formatting | bytes 16777216

commit v5 on v4

--- a/solution.py
+++ b/solution.py
@@ -8,6 +8,7 @@
 from jax.sharding import PartitionSpec as P
 
 SLOTS = 8
+SENDS = 4
 AHEAD = 2
 MESH = pl.DeviceIdType.MESH
 
@@ -29,8 +30,8 @@
 
 def kernel(shape, z_hbm, v_ref, t_ref, out_ref, zbuf, vbuf, tbuf, stage, acc, psend, precv, *sems):
     groups, A, B, zone, tile = shape
-    recv, su, sd, sy, sc, lsem, zsem, psnd, prcv, town, tsnd, trcv = sems[:12]
-    lsnd, lrcv, gsnd, grcv = sems[12:]
+    recv, rside, rpair, su, sd, sy, sc, tu, td, ty, tc, tr = sems[:12]
+    lsem, zsem, psnd, prcv, town, tsnd, trcv, lsnd, lrcv, gsnd, grcv = sems[12:]
     panels, H, sub, rows = v_ref.shape
     members = 2 * A * B
     ring = vbuf.shape[0]
@@ -55,19 +56,26 @@
     def index(aa, bb, cc):
         return (aa * B + bb) * 2 + cc
 
-    def place(u, owner, q, start=0):
-        if q == 2:
-            return tbuf.at[mine, :, owner]
-        span = pl.ds(cut, rows - cut) if q else pl.ds(start, cut - start)
-        return vbuf.at[lax.rem(u // H, ring), lax.rem(u, H), owner, :, span]
-
-    def sized(u, q, body):
-        if zone and q == 0:
+    def place(u, owner, lo, hi):
+        return vbuf.at[lax.rem(u // H, ring), lax.rem(u, H), owner, :, pl.ds(lo, hi - lo)]
+
+    def sized(u, body):
+        if zone:
             pl.when(u < early)(lambda: body(half))
             pl.when(u >= early)(lambda: body(0))
         else:
             body(0)
 
+    def landed(spot, sem):
+        pltpu.make_async_remote_copy(
+            src_ref=spot,
+            dst_ref=spot,
+            send_sem=sc.at[0, 0],
+            recv_sem=sem,
+            device_id={"col": index(a, b, 1 - c)},
+            device_id_type=MESH,
+        ).wait_recv()
+
     def source(u, span):
         return v_ref.at[panels - 1 - u // H, lax.rem(u, H), :, span]
 
@@ -83,109 +91,64 @@
         borrowed = (my_row == 0) & (u < early)
         pl.when(borrowed)(lambda: body(staged(u)))
 
-    def landed(u, owner, q):
-        sl = lax.rem(u, SLOTS)
-
-        def wait(start):
-            spot = place(u, owner, q, start)
-            pltpu.make_async_remote_copy(
-                src_ref=spot,
-                dst_ref=spot,
-                send_sem=sc.at[sl, q, 0],
-                recv_sem=recv.at[sl, q, owner],
-                device_id={"col": index(a, b, 1 - c)},
-                device_id_type=MESH,
-            ).wait_recv()
-
-        sized(u, q, wait)
-
     def hop(u, h, go, stages=(0, 1)):
         sl = lax.rem(u, SLOTS)
-
-        def move(owner, q, own, target, sem, part=None):
-            def copy(src, dst):
-                return pltpu.make_async_remote_copy(
-                    src_ref=src,
-                    dst_ref=dst,
-                    send_sem=sem,
-                    recv_sem=recv.at[sl, q, owner],
-                    device_id={"col": target},
-                    device_id_type=MESH,
-                )
-
-            def whole(start):
-                spot = place(u, owner, q, start)
-                if not go:
-                    copy(spot, spot).wait_send()
-                elif q == 2 and own:
-                    copy(t_ref.at[mine], spot).start()
-                elif own:
-                    span = pl.ds(cut, rows - cut) if q else pl.ds(start, cut - start)
-                    copy(source(u, span), spot).start()
+        ts = lax.rem(u + (h - 1 if h else SENDS - AHEAD), SENDS)
+
+        def copy(src, dst, target, send_sem, recv_sem):
+            return pltpu.make_async_remote_copy(
+                src_ref=src,
+                dst_ref=dst,
+                send_sem=send_sem,
+                recv_sem=recv_sem,
+                device_id={"col": target},
+                device_id_type=MESH,
+            )
+
+        def move(owner, stop, target, send_sem, recv_sem):
+            def part(src, lo, hi):
+                copy(src, place(u, owner, lo, hi), target, send_sem, recv_sem).start()
+
+            def fresh(lo, hi):
+                part(source(u, pl.ds(lo, hi - lo)), lo, hi)
+
+            def passed(lo, hi):
+                spot = place(u, owner, lo, hi)
+                one = copy(spot, spot, target, send_sem, recv_sem)
+                one.start() if go else one.wait_send()
+
+            if not go or h:
+                if stop is None:
+                    passed(cut, rows)
                 else:
-                    copy(spot, spot).start()
-
-            if part == "mid":
-                lent(u, lambda src: copy(src, slot_of(u, mid)).start())
-            elif zone and go and own and q == 0:
+                    sized(u, lambda start: passed(start, stop))
+            elif stop is None:
+                if 0 in stages:
+                    fresh(cut, rows)
+            elif zone:
                 borrowed = (my_row == 0) & (u < early)
-                pl.when(borrowed)(lambda: whole(zone))
-                pl.when(jnp.logical_not(borrowed) & (u < early))(lambda: whole(half))
-                pl.when(u >= early)(lambda: whole(0))
-            else:
-                sized(u, q, whole)
-
-        def arrive(owner, q):
-            if go:
-                landed(u, owner, q)
-
-        def along(sg, owner, q, own, cid, part=None):
+                if 0 in stages:
+                    pl.when(borrowed)(lambda: fresh(zone, stop))
+                    pl.when(jnp.logical_not(borrowed) & (u < early))(lambda: fresh(half, stop))
+                    pl.when(u >= early)(lambda: fresh(0, stop))
+                if 1 in stages:
+                    pl.when(borrowed)(lambda: part(staged(u), half, zone))
+            elif 0 in stages:
+                fresh(0, stop)
+
+        def move_factor(owner, target, send_sem, recv_sem):
+            spot = tbuf.at[mine, :, owner]
+            one = copy(spot if h else t_ref.at[mine], spot, target, send_sem, recv_sem)
+            one.start() if go else one.wait_send()
+
+        def both(sg, body):
             if sg >= 0:
-
-                @pl.when(a < A - 1)
-                def _():
-                    move(owner, q, own, index(a + 1, b, c), su.at[sl, q, cid], part)
-
+                pl.when(a < A - 1)(lambda: body(index(a + 1, b, c), 0))
             if sg <= 0:
-
-                @pl.when(a > 0)
-                def _():
-                    move(owner, q, own, index(a - 1, b, c), sd.at[sl, q, cid], part)
-
-        def across(owner, q, own, at, part=None):
-            slot = (at, A, A + 1 + at)[q]
-            for j in range(1, B):
-                move(owner, q, own, index(a, lax.rem(b + j, B), c), sy.at[sl, slot, j - 1], part)
-
-        def over(owner, q, own, cid, part=None):
-            move(owner, q, own, index(a, b, 1 - c), sc.at[sl, q, cid], part)
-
-        def factors(body):
-            pl.when(u == 0)(body)
+                pl.when(a > 0)(lambda: body(index(a - 1, b, c), 1))
 
         def signs(d):
             return (1, -1) if d else (0,)
-
-        def spread(q, part=None):
-            cid = a * B + b
-            along(0, me, q, True, cid, part)
-            across(me, q, True, a, part)
-            over(me, q, True, cid, part)
-
-        if h == 0:
-            if 0 in stages:
-                across(me, 1, True, a)
-                along(0, me, 0, True, a * B + b)
-                along(0, me, 1, True, a * B + b)
-                across(me, 0, True, a)
-                over(me, 0, True, a * B + b)
-                over(me, 1, True, a * B + b)
-                factors(lambda: spread(2))
-            if 1 in stages and go:
-                if zone:
-                    spread(0, "mid")
-                own_vectors(u)
-            return
 
         def facing(d, body):
             if d < A:
@@ -196,49 +159,62 @@
                     else:
                         pl.when((at >= 0) & (at < A))(functools.partial(body, sg, at))
 
+        def forward(sg, at):
+            owner, cid = index(at, b, c), at * B + b
+            both(sg, lambda to, way: move(owner, rows, to, (su, sd)[way].at[ts, at * B], recv.at[sl, cid]))
+            for j in range(1, B):
+                to = index(a, lax.rem(b + j, B), c)
+                if h == 0:
+                    side = at * (B - 1) + (B - j - 1)
+                    move(owner, None, to, sy.at[ts, A, j - 1], rside.at[sl, side])
+                move(owner, cut, to, sy.at[ts, at, j - 1], recv.at[sl, cid])
+            move(owner, rows, index(a, b, 1 - c), sc.at[ts, cid], rpair.at[sl, cid])
+
+            if 0 in stages:
+
+                @pl.when(u == 0)
+                def _():
+                    both(sg, lambda to, way: move_factor(owner, to, (tu, td)[way].at[at], tr.at[0, cid]))
+                    for j in range(1, B):
+                        to = index(a, lax.rem(b + j, B), c)
+                        move_factor(owner, to, ty.at[at, j - 1], tr.at[0, cid])
+                    move_factor(owner, index(a, b, 1 - c), tc.at[cid], tr.at[1, cid])
+
         def straight(sg, at):
             owner, cid = index(at, b, c), at * B + b
-            arrive(owner, 0)
-            along(sg, owner, 0, False, cid)
-            across(owner, 0, False, at)
-            over(owner, 0, False, cid)
-
-            @factors
-            def _():
-                arrive(owner, 2)
-                along(sg, owner, 2, False, cid)
-                across(owner, 2, False, at)
-                over(owner, 2, False, cid)
+            if go:
+                sized(u, lambda start: landed(place(u, owner, start, rows), recv.at[sl, cid]))
+                pl.when(u == 0)(lambda: landed(tbuf.at[mine, :, owner], tr.at[0, cid]))
+            forward(sg, at)
 
         def turned(sg, at):
             for j in range(1, B):
-                bb = lax.rem(b + j, B)
-                owner, cid = index(at, bb, c), at * B + bb
-                arrive(owner, 1)
-                along(sg, owner, 1, False, cid)
-                over(owner, 1, False, cid)
-
-        def beside(sg, at):
-            owner, cid = index(at, b, c), at * B + b
-            arrive(owner, 1)
-            along(sg, owner, 1, False, cid)
-            over(owner, 1, False, cid)
+                owner, side = index(at, lax.rem(b + j, B), c), at * (B - 1) + (j - 1)
+                if go:
+                    landed(place(u, owner, cut, rows), rside.at[sl, side])
+                both(sg, lambda to, way: move(owner, None, to, (su, sd)[way].at[ts, at * B + j], rside.at[sl, side]))
 
         def crossed(sg, at):
             for j in range(1, B):
                 bb = lax.rem(b + j, B)
                 owner, cid = index(at, bb, c), at * B + bb
-                arrive(owner, 0)
-                over(owner, 0, False, cid)
-
-                @factors
+                if go:
+                    sized(u, lambda start: landed(place(u, owner, start, cut), recv.at[sl, cid]))
+                    pl.when(u == 0)(lambda: landed(tbuf.at[mine, :, owner], tr.at[0, cid]))
+                move(owner, rows, index(a, b, 1 - c), sc.at[ts, cid], rpair.at[sl, cid])
+
+                @pl.when(u == 0)
                 def _():
-                    arrive(owner, 2)
-                    over(owner, 2, False, cid)
+                    move_factor(owner, index(a, b, 1 - c), tc.at[cid], tr.at[1, cid])
+
+        if h == 0:
+            forward(0, a)
+            if 1 in stages and go:
+                own_vectors(u)
+            return
 
         facing(h, straight)
         facing(h - 1, turned)
-        facing(h, beside)
         facing(h - 1, crossed)
 
     def pass_factors(j):
@@ -257,8 +233,8 @@
     def settle(u):
         for at in range(A):
             for bb in range(B):
-                for q in range(2):
-                    landed(u, index(at, bb, 1 - c), q)
+                owner, sem = index(at, bb, 1 - c), rpair.at[lax.rem(u, SLOTS), at * B + bb]
+                sized(u, lambda start: landed(place(u, owner, start, rows), sem))
 
         if zone:
 
@@ -280,7 +256,7 @@
         def _():
             for at in range(A):
                 for bb in range(B):
-                    landed(u, index(at, bb, 1 - c), 2)
+                    landed(tbuf.at[mine, :, index(at, bb, 1 - c)], tr.at[1, at * B + bb])
             own_factors().wait()
             for j in range(1, groups):
                 pass_factors(j).start()
@@ -449,7 +425,7 @@
     def slot(t, _):
         w = t - A
 
-        @pl.when(w >= 0)
+        @pl.when((w >= 0) & (w < units))
         def _():
             i, h = w // H, lax.rem(w, H)
 
@@ -480,19 +456,22 @@
         def _():
             settle(v)
 
-        @pl.when(w >= 0)
-        def _():
-            for h in range(A + 1):
-                hop(w, h, False)
-            if zone:
-
-                @pl.when((my_row == 0) & (w < early))
-                def _():
-                    hand(w).wait_send()
+        for h in range(A + 1):
+            u = t - (SENDS - 1) - (h - 1 if h else -AHEAD)
+
+            @pl.when((u >= 0) & (u < units))
+            def _(u=u, h=h):
+                hop(u, h, False)
+
+        if zone:
+
+            @pl.when((my_row == 0) & (w >= 0) & (w < early))
+            def _():
+                hand(w).wait_send()
 
         return 0
 
-    lax.fori_loop(0, units + A, slot, 0)
+    lax.fori_loop(0, units + A + SENDS - 2, slot, 0)
     update(jnp.int32(panels - 1), True)
     if zone:
 
@@ -537,11 +516,18 @@
             pltpu.VMEM((width, columns), jnp.float32),
             pltpu.VMEM((2 * H, members * sub, columns), jnp.float32),
             pltpu.VMEM((2 * H, others, members * sub, columns), jnp.float32),
-            dma((SLOTS, 3, members)),
-            dma((SLOTS, 3, chips)),
-            dma((SLOTS, 3, chips)),
-            dma((SLOTS, 2 * A + 1, max(B - 1, 1))),
-            dma((SLOTS, 3, chips)),
+            dma((SLOTS, chips)),
+            dma((SLOTS, A * max(B - 1, 1))),
+            dma((SLOTS, chips)),
+            dma((SENDS, chips)),
+            dma((SENDS, chips)),
+            dma((SENDS, A + 1, max(B - 1, 1))),
+            dma((SENDS, chips)),
+            dma((A,)),
+            dma((A,)),
+            dma((A, max(B - 1, 1))),
+            dma((chips,)),
+            dma((2, chips)),
             dma((SLOTS,)),
             dma,
             dma((2 * H, others)),

time: 360 us -> 354 us (0.983)
  Pallas kernels: 353 us -> 346 us
    pallas_call x1, Pallas kernels: 353 us -> 346 us  [local(): pl.pallas_call(functools.partial(kernel, (groups, A, B, zone, tile)), out...]
where the time goes in v5:
time: 354 us
  Pallas kernels  346 us (98%)
  local copies, waits for them, and re-layouts  7.32 us (2%)
    pallas_call x1, Pallas kernels, local(): pl.pallas_call(functools.partial(kernel, (groups, A, B, zone, tile)), out...  346 us
    unnamed x1, local copies, waits for them, and re-layouts  7.32 us

profile of v5, /device:TPU:0, one launch (start us, length us, event | category | flops | bytes accessed | tf_op | source)
XLA Modules:
  0.0 353.6 jit_solution(7899108025746781728)
XLA Ops:
  0.0 346.3 %shard_map.37 = f32[8192,256]{1,0:T(8,128)} custom-call(f32[8192,256]{1,0:T(8,128)} %z_hbm.1, f32[8,2,8,8192]{3,2,1,0:T(8,128)} %bitcast.6, f32[8,2,8,256]{3,2,1,0:T(8,128)} %bitcast.7), custom_call_target="tpu_custom_call" | custom-call | tf_op jit(solution)/shard_map/pallas_call | solution.py:506
  346.3 7.3 %copy.5 = f32[8192,256]{1,0:T(8,128)} copy(f32[8192,256]{1,0:T(8,128)} %shard_map.37) | data formatting | bytes 16777216

commit v6 on v5

--- a/solution.py
+++ b/solution.py
@@ -44,6 +44,10 @@
     side = min(max((tiles * spare + whole // 2) // whole, 1), tiles - 1)
     cut = (tiles - side) * 128
     half = zone // 2
+
+    def is_early(u):
+        return (u > 0) & (u < early)
+
     floor = zone // width
     early = (panels - floor) * H if zone else 0
     me = lax.axis_index("col")
@@ -61,8 +65,8 @@
 
     def sized(u, body):
         if zone:
-            pl.when(u < early)(lambda: body(half))
-            pl.when(u >= early)(lambda: body(0))
+            pl.when(is_early(u))(lambda: body(half))
+            pl.when(jnp.logical_not(is_early(u)))(lambda: body(0))
         else:
             body(0)
 
@@ -88,7 +92,7 @@
     low, mid, high = pl.ds(0, half), pl.ds(half, zone - half), pl.ds(zone, rows - zone)
 
     def lent(u, body):
-        borrowed = (my_row == 0) & (u < early)
+        borrowed = (my_row == 0) & (is_early(u))
         pl.when(borrowed)(lambda: body(staged(u)))
 
     def hop(u, h, go, stages=(0, 1)):
@@ -126,11 +130,11 @@
                 if 0 in stages:
                     fresh(cut, rows)
             elif zone:
-                borrowed = (my_row == 0) & (u < early)
+                borrowed = (my_row == 0) & (is_early(u))
                 if 0 in stages:
                     pl.when(borrowed)(lambda: fresh(zone, stop))
-                    pl.when(jnp.logical_not(borrowed) & (u < early))(lambda: fresh(half, stop))
-                    pl.when(u >= early)(lambda: fresh(0, stop))
+                    pl.when(jnp.logical_not(borrowed) & (is_early(u)))(lambda: fresh(half, stop))
+                    pl.when(jnp.logical_not(is_early(u)))(lambda: fresh(0, stop))
                 if 1 in stages:
                     pl.when(borrowed)(lambda: part(staged(u), half, zone))
             elif 0 in stages:
@@ -238,11 +242,11 @@
 
         if zone:
 
-            @pl.when(u >= early)
+            @pl.when(jnp.logical_not(is_early(u)))
             def _():
                 own_arrived(u, pl.ds(0, rows))
 
-            @pl.when(u < early)
+            @pl.when(is_early(u))
             def _():
                 own_arrived(u, pl.ds(half, rows - half))
 
@@ -268,10 +272,10 @@
         if zone:
             lent(u, lambda src: fetch_own(src, mid))
             rest = pl.ds(half, rows - half)
-            borrowed = (my_row == 0) & (u < early)
+            borrowed = (my_row == 0) & (is_early(u))
             pl.when(borrowed)(lambda: fetch_own(source(u, high), high))
-            pl.when(jnp.logical_not(borrowed) & (u < early))(lambda: fetch_own(source(u, rest), rest))
-            pl.when(u >= early)(lambda: fetch_own(source(u, pl.ds(0, rows)), pl.ds(0, rows)))
+            pl.when(jnp.logical_not(borrowed) & (is_early(u)))(lambda: fetch_own(source(u, rest), rest))
+            pl.when(jnp.logical_not(is_early(u)))(lambda: fetch_own(source(u, pl.ds(0, rows)), pl.ds(0, rows)))
         else:
             fetch_own(source(u, pl.ds(0, rows)), pl.ds(0, rows))
 
@@ -300,7 +304,7 @@
         )
 
     def begin(u):
-        return jnp.where((my_row == 0) & (u < early), 1, 0) if zone else 0
+        return jnp.where((my_row == 0) & (is_early(u)), 1, 0) if zone else 0
 
     def swap_factors():
         for j in range(1, groups):
@@ -330,7 +334,7 @@
         sl = lax.rem(u, 2 * H)
         if zone:
 
-            @pl.when((my_row == 1) & (u < early))
+            @pl.when((my_row == 1) & (is_early(u)))
             def _():
                 hand(u).wait_recv()
 
@@ -384,7 +388,7 @@
 
             return 0
 
-        lax.fori_loop(0 if last else begin(i * H), rows // tile, body, 0)
+        lax.fori_loop(0 if last else begin(i * H + H - 1), rows // tile, body, 0)
 
     barrier = pltpu.get_barrier_semaphore()
 
@@ -408,7 +412,8 @@
         def _():
             lend().start()
 
-    for u in range(AHEAD):
+    hop(jnp.int32(0), 0, True)
+    for u in range(1, AHEAD):
         hop(jnp.int32(u), 0, True, (0,))
     fetch.start()
     own_factors().start()
@@ -418,7 +423,7 @@
         def _():
             lend().wait_recv()
 
-    for u in range(AHEAD):
+    for u in range(1, AHEAD):
         hop(jnp.int32(u), 0, True, (1,))
     fetch.wait()
 
@@ -465,7 +470,7 @@
 
         if zone:
 
-            @pl.when((my_row == 0) & (w >= 0) & (w < early))
+            @pl.when((my_row == 0) & is_early(w))
             def _():
                 hand(w).wait_send()
 

time: 354 us -> 353 us (level)
  no operation moved by 1% of the time
where the time goes in v6:
time: 353 us
  Pallas kernels  345 us (98%)
  local copies, waits for them, and re-layouts  7.32 us (2%)
    pallas_call x1, Pallas kernels, local(): pl.pallas_call(functools.partial(kernel, (groups, A, B, zone, tile)), out...  345 us
    unnamed x1, local copies, waits for them, and re-layouts  7.32 us

profile of v6, /device:TPU:0, one launch (start us, length us, event | category | flops | bytes accessed | tf_op | source)
XLA Modules:
  0.0 352.8 jit_solution(13580112937524937892)
XLA Ops:
  0.0 345.5 %shard_map.37 = f32[8192,256]{1,0:T(8,128)} custom-call(f32[8192,256]{1,0:T(8,128)} %z_hbm.1, f32[8,2,8,8192]{3,2,1,0:T(8,128)} %bitcast.6, f32[8,2,8,256]{3,2,1,0:T(8,128)} %bitcast.7), custom_call_target="tpu_custom_call" | custom-call | tf_op jit(solution)/shard_map/pallas_call | solution.py:511
  345.5 7.3 %copy.5 = f32[8192,256]{1,0:T(8,128)} copy(f32[8192,256]{1,0:T(8,128)} %shard_map.37) | data formatting | bytes 16777216

commit v7 on v6

--- a/solution.py
+++ b/solution.py
@@ -8,7 +8,7 @@
 from jax.sharding import PartitionSpec as P
 
 SLOTS = 8
-SENDS = 4
+SENDS = 3
 AHEAD = 2
 MESH = pl.DeviceIdType.MESH
 
@@ -25,7 +25,7 @@
         )
 
     (lh, ll), (rh, rl) = left, right
-    return one(lh, rh) + (one(ll, rh) + one(lh, rl))
+    return one(jnp.concatenate([lh, ll, lh], left_axis), jnp.concatenate([rh, rh, rl], right_axis))
 
 
 def kernel(shape, z_hbm, v_ref, t_ref, out_ref, zbuf, vbuf, tbuf, stage, acc, psend, precv, *sems):

time: 353 us -> 353 us (level)
  no operation moved by 1% of the time
where the time goes in v7:
time: 353 us; the launch traced here: 352 us
  Pallas kernels  345 us (98%)
  local copies, waits for them, and re-layouts  7.32 us (2%)
    pallas_call x1, Pallas kernels, local(): pl.pallas_call(functools.partial(kernel, (groups, A, B, zone, tile)), out...  345 us
    unnamed x1, local copies, waits for them, and re-layouts  7.32 us

profile of v7, /device:TPU:0, one launch (start us, length us, event | category | flops | bytes accessed | tf_op | source)
XLA Modules:
  0.0 352.4 jit_solution(9845187524033692658)
XLA Ops:
  0.0 345.1 %shard_map.37 = f32[8192,256]{1,0:T(8,128)} custom-call(f32[8192,256]{1,0:T(8,128)} %z_hbm.1, f32[8,2,8,8192]{3,2,1,0:T(8,128)} %bitcast.6, f32[8,2,8,256]{3,2,1,0:T(8,128)} %bitcast.7), custom_call_target="tpu_custom_call" | custom-call | tf_op jit(solution)/shard_map/pallas_call | solution.py:511
  345.1 7.3 %copy.5 = f32[8192,256]{1,0:T(8,128)} copy(f32[8192,256]{1,0:T(8,128)} %shard_map.37) | data formatting | bytes 16777216
